TPU v7x, 32 devices: a whole 2x2x4 slice. The times are simulated.
32 devices in a mesh: groups: 2 (over y), expert: 4 (over z), tensor: 4 (over x, core).
Axes of the slice: x: 2, y: 2, z: 4, core: 2. Of those that a mesh axis runs over, the one named last changes fastest.
Arguments:
- kv_prefill: bfloat16 [32, 512, 2, 1024], P('groups', 'expert', None, 'tensor'), parts along dimension 0, may hold values from -8 to 8
- slot_of: int32 [32], P('groups'), parts along dimension 0, may hold values from 0 to 15, as said below
- lengths: int32 [32], P('groups'), parts along dimension 0, may hold values from 2 to 512
- query: bfloat16 [32, 4096], P(('groups', 'expert'), 'tensor'), parts along dimension 0, may hold values from -100 to 100
- new_kv: bfloat16 [32, 2, 1024], P(('groups', 'expert'), None, 'tensor'), parts along dimension 0, may hold values from -6 to 6
- wo: bfloat16 [4096, 4096], P('tensor', 'expert'), may hold values from -0.09375 to 0.09375
- resid: bfloat16 [32, 4096], P('groups', 'expert'), parts along dimension 0, may hold values from -60 to 60
- norm_gain: bfloat16 [4096], P('expert'), may hold values from 0.25 to 1.75
- expert_ids: int32 [32, 2], P('groups'), parts along dimension 0, may hold values from 0 to 3, all different within a row; in each aligned block of 16 rows (0 to 15, 16 to 31, ...) at most 12 rows name the same one
- gate_logits: float32 [32, 2], P('groups'), parts along dimension 0, may hold values from -6 to 6
- gate_weight_slabs: bfloat16 [4, 4096, 8192], P('expert', None, 'tensor'), may hold values from -0.09375 to 0.09375
- w_up: bfloat16 [4, 4096, 8192], P('expert', None, 'tensor'), may hold values from -0.09375 to 0.09375
- w_down: bfloat16 [4, 8192, 4096], P('expert', 'tensor'), may hold values from -0.0625 to 0.0625
Outputs:
- attn_out: bfloat16 [32, 4096], P('groups', 'expert'), parts along dimension 0
- moe_out: bfloat16 [32, 4096], P(('groups', 'tensor'), 'expert'), parts along dimension 0
There are 2 independent parts, one for each index of `groups`. A program takes and returns all parts, laid end to end along the dimension named above; an argument that names none is the same for every part. Nothing has to cross between parts.
Inputs may be any that keep to these rules, and one draw needn't show every extreme that they name: `slot_of`: a permutation of 0 to 15. `expert_ids`: each expert is named by at most 12 tokens, one of them by exactly 12; no token names an expert twice.
All inputs are finite; a program needn't handle non-finite values.
Results may differ from a plain program's by a relative error of at most 0.023.
Values may be sent and summed in bfloat16 or wider, within the bound.
A program may use at most 128 MiB of HBM per device.

v0:
```python
import math

import jax
import jax.numpy as jnp
from jax import lax
from jax.sharding import PartitionSpec as P

D = 4096
HEADS = 32
KVH = 8
HD = 128
EXPERTS = 4


EPSILON = 1e-05
MASKED = -1e30


def cache_partial(query_vectors, key_rows, value_rows, live_mask, logit_scale_factor):
    scores = (
        jnp.einsum("rkqd,rpkd->rkqp", query_vectors, key_rows, preferred_element_type=jnp.float32)
        * logit_scale_factor
    )
    mask_rows = live_mask[:, None, None, :]
    scores = jnp.where(mask_rows, scores, MASKED)
    peak_value = jnp.max(scores, axis=-1)
    exp_weights = jnp.where(mask_rows, jnp.exp(scores - peak_value[..., None]), 0.0)
    denominator = jnp.sum(exp_weights, axis=-1)
    summed = jnp.einsum(
        "rkqp,rpkd->rkqd",
        exp_weights.astype(jnp.bfloat16),
        value_rows,
        preferred_element_type=jnp.float32,
    )
    return (peak_value, denominator, summed)


def combine(earlier, latter):
    peak_value = jnp.maximum(earlier[0], latter[0])
    weight_left = jnp.exp(earlier[0] - peak_value)
    weight_right = jnp.exp(latter[0] - peak_value)
    denominator = earlier[1] * weight_left + latter[1] * weight_right
    summed = earlier[2] * weight_left[..., None] + latter[2] * weight_right[..., None]
    return (peak_value, denominator, summed)


def finish(state, query_vectors, new_rows, logit_scale_factor):
    row_count, kv_local, group_size, head_size = query_vectors.shape
    fresh_key_rows = new_rows[:, 0, :].reshape(row_count, kv_local, head_size)
    new_values = new_rows[:, 1, :].reshape(row_count, kv_local, 1, head_size).astype(jnp.float32)
    self_score_value = (
        jnp.einsum(
            "rkqd,rkd->rkq", query_vectors, fresh_key_rows, preferred_element_type=jnp.float32
        )
        * logit_scale_factor
    )
    own_state = (
        self_score_value,
        jnp.ones_like(self_score_value),
        jnp.broadcast_to(new_values, query_vectors.shape),
    )
    peak_value, denominator, summed = combine(state, own_state)
    return (
        (summed / denominator[..., None])
        .reshape(row_count, kv_local * group_size * head_size)
        .astype(jnp.bfloat16)
    )


def shards(
    kv_prefill,
    slot_of,
    lengths,
    query,
    new_kv,
    wo,
    resid,
    norm_gain,
    expert_ids,
    gate_logits,
    gate_weight_slabs,
    w_up,
    w_down,
):
    axis_count = lax.axis_size("expert")
    my_index = lax.axis_index("expert")
    kv_local = kv_prefill.shape[3] // HD
    group_size = HEADS // KVH
    logit_scale_factor = 1.0 / math.sqrt(HD)
    seq_count = query.shape[0]
    total_rows = lengths.shape[0]
    ordered = jnp.take(kv_prefill, slot_of, axis=0)
    own_cache = lax.all_to_all(ordered, "expert", split_axis=0, concat_axis=1, tiled=True)
    positions = own_cache.shape[1]
    key_rows = own_cache[:, :, 0, :].reshape(seq_count, positions, kv_local, HD)
    value_rows = own_cache[:, :, 1, :].reshape(seq_count, positions, kv_local, HD)
    own_lengths = lax.dynamic_slice_in_dim(lengths, my_index * seq_count, seq_count)
    live_mask = jnp.arange(positions, dtype=jnp.int32)[None, :] < own_lengths[:, None]
    query_vectors = query.reshape(seq_count, kv_local, group_size, HD)
    state = cache_partial(query_vectors, key_rows, value_rows, live_mask, logit_scale_factor)
    context = finish(state, query_vectors, new_kv, logit_scale_factor)
    partial_out = jnp.dot(
        lax.all_gather(context, "expert", axis=0, tiled=True),
        wo,
        preferred_element_type=jnp.float32,
    )
    attention = lax.psum(partial_out.astype(jnp.bfloat16), "tensor")
    hidden_activation = resid.astype(jnp.float32) + attention.astype(jnp.float32)
    squares = lax.psum(jnp.sum(hidden_activation * hidden_activation, axis=1), "expert")
    normed = (
        hidden_activation
        * lax.rsqrt(squares / D + EPSILON)[:, None]
        * norm_gain.astype(jnp.float32)[None, :]
    ).astype(jnp.bfloat16)
    first_share = 1.0 / (1.0 + jnp.exp(gate_logits[:, 1] - gate_logits[:, 0]))
    shares = jnp.stack([first_share, 1.0 - first_share], axis=1)
    sharing = axis_count // EXPERTS
    my_expert = my_index // sharing
    mine_mask = expert_ids == my_expert
    mix_mine = jnp.sum(jnp.where(mine_mask, shares, 0.0), axis=1)
    gate_slab = gate_weight_slabs[0]
    up_slab = w_up[0]
    down_slab = w_down[0]
    capacity = 3 * total_rows // 4
    expert_range = jnp.arange(EXPERTS, dtype=jnp.int32)
    picked = jnp.any(expert_ids[:, :, None] == expert_range[None, None, :], axis=1).astype(
        jnp.int32
    )
    rank_of = jnp.cumsum(picked, axis=0) - 1
    slot_range = jnp.arange(capacity, dtype=jnp.int32)
    slot_hits = (picked[:, :, None] > 0) & (rank_of[:, :, None] == slot_range[None, None, :])
    token_range = jnp.arange(total_rows, dtype=jnp.int32)[:, None, None]
    token_table = jnp.sum(jnp.where(slot_hits, token_range, 0), axis=0)
    token_table = token_table + jnp.where(jnp.any(slot_hits, axis=0), 0, total_rows)
    padded_rows = jnp.concatenate([normed, jnp.zeros((1, normed.shape[1]), jnp.bfloat16)], axis=0)
    blocks = jnp.take(padded_rows, token_table, axis=0)
    outgoing = jnp.repeat(blocks, sharing, axis=0)
    arrived = lax.all_to_all(outgoing, "expert", split_axis=0, concat_axis=2, tiled=True)[0]
    gate_sum = jnp.dot(arrived, gate_slab, preferred_element_type=jnp.float32)
    up_sum = jnp.dot(arrived, up_slab, preferred_element_type=jnp.float32)
    activated = (jax.nn.silu(gate_sum) * up_sum).astype(jnp.bfloat16)
    produced = jnp.dot(activated, down_slab, preferred_element_type=jnp.float32)
    own_picked = jnp.any(mine_mask, axis=1)
    own_rank = jnp.sum(jnp.where(expert_range[None, :] == my_expert, rank_of, 0), axis=1)
    slot_index = jnp.where(own_picked, own_rank, capacity)
    padded_out = jnp.concatenate([produced, jnp.zeros((1, produced.shape[1]), jnp.float32)], axis=0)
    contrib = jnp.take(padded_out, slot_index, axis=0) * mix_mine[:, None]
    column_part = lax.psum_scatter(
        contrib.astype(jnp.bfloat16), "expert", scatter_dimension=1, tiled=True
    )
    summed_out = lax.psum_scatter(column_part, "tensor", scatter_dimension=0, tiled=True).astype(
        jnp.float32
    )
    moe_out = summed_out.astype(jnp.bfloat16)
    return (attention, moe_out)


def solution(mesh):
    return jax.shard_map(
        shards,
        mesh=mesh,
        in_specs=(
            P("groups", "expert", None, "tensor"),
            P("groups"),
            P("groups"),
            P(("groups", "expert"), "tensor"),
            P(("groups", "expert"), None, "tensor"),
            P("tensor", "expert"),
            P("groups", "expert"),
            P("expert"),
            P("groups", None),
            P("groups", None),
            P("expert", None, "tensor"),
            P("expert", None, "tensor"),
            P("expert", "tensor", None),
        ),
        out_specs=(P("groups", "expert"), P(("groups", "tensor"), "expert")),
        check_vma=False,
    )
```

profile of v0, /device:TPU:0, one launch (start us, length us, event | category | flops | bytes accessed | tf_op | source)
XLA Modules:
  0.0 184.8 jit_solution(8807511361082113522)
XLA Ops:
  7.2 0.8 compare_select_fusion.4
  8.0 0.7 compare_and_fusion.2
  8.8 5.9 %gather_fusion = bf16[16,128,2,256]{3,2,1,0:T(2,128)(2,1)} fusion(bf16[16,128,2,256]{3,2,1,0:T(2,128)(2,1)S(1)} %copy-done, s32[1024]{0:T(1024)S(1)} %pad_clamp_fusion.2), kind=kCustom, calls=%fused_computation | custom fusion | bytes 4194368 | tf_op jit(solution)/shard_map/jit(_take)/gather | solution.py:92
  14.7 4.8 %broadcast_select_fusion = bf16[16,128,2,256]{3,2,1,0:T(2,128)(2,1)} fusion(bf16[16,128,2,256]{3,2,1,0:T(2,128)(2,1)} %gather_fusion, pred[16]{0:T(512)(128)(4,1)S(1)} %compare_and_fusion.2), kind=kLoop, calls=%fused_computation.9 | loop fusion | flops 1048576 | bytes 4194320 | tf_op jit(solution)/shard_map/jit(_take)/select_n | solution.py:92
  19.5 6.5 %all-to-all-start = ((bf16[16,128,2,256]{3,2,1,0:T(2,128)(2,1)}), bf16[16,128,2,256]{3,2,1,0:T(2,128)(2,1)S(1)}, u32[]{:S(2)}, u32[]{:S(2)}) async-start(bf16[16,128,2,256]{3,2,1,0:T(2,128)(2,1)} %broadcast_select_fusion), calls=%async_computation | async-start | bytes 4194304 | tf_op jit(solution)/shard_map/all_to_all | solution.py:93
  26.6 0.3 fusion.32
  26.9 0.3 select_reduce_fusion
  27.8 46.4 %all-to-all-done = bf16[16,128,2,256]{3,2,1,0:T(2,128)(2,1)S(1)} async-done(((bf16[16,128,2,256]{3,2,1,0:T(2,128)(2,1)}), bf16[16,128,2,256]{3,2,1,0:T(2,128)(2,1)S(1)}, u32[]{:S(2)}, u32[]{:S(2)}) %all-to-all-start) | async-done | bytes 2097184 | tf_op jit(solution)/shard_map/all_to_all | solution.py:93
  74.2 0.4 copy.49
  74.8 1.1 fusion.45
  75.9 1.5 copy.53
  77.4 0.5 copy.51
  77.9 0.3 fusion.46
  78.3 0.2 fusion.25
  78.5 0.4 fusion.16
  78.9 13.2 %all-gather = bf16[4,4,1024]{2,1,0:T(4,128)(2,1)S(1)} all-gather(bf16[1,4,1024]{2,1,0:T(4,128)(2,1)S(1)} %reshape.151), channel_id=1, replica_groups=mesh['groups'=2,'expert'=4,'tensor'=4] {'expert'}, dimensions={0}, use_global_device_ids=true | all-gather | bytes 40960 | tf_op jit(solution)/shard_map/all_gather | solution.py:103
  92.1 2.0 %convolution_convert_fusion = bf16[16,1024]{1,0:T(8,128)(2,1)S(1)} fusion(bf16[16,1024]{1,0:T(8,128)(2,1)S(1)} %reshape.152, bf16[1024,1024]{1,0:T(8,128)(2,1)} %param.18), kind=kOutput, calls=%fused_computation.15 | convolution fusion | flops 33570816 | bytes 2162688 | tf_op jit(solution)/shard_map/dot_general | solution.py:102
  94.1 10.3 %psum.14 = bf16[16,1024]{1,0:T(8,128)(2,1)S(1)} all-reduce(bf16[16,1024]{1,0:T(8,128)(2,1)S(1)} %convolution_convert_fusion), channel_id=1, replica_groups=mesh['groups'=2,'expert'=4,'tensor'=4] {'tensor'}, use_global_device_ids=true, to_apply=%region_2.3 | all-reduce | flops 16384 | bytes 65536 | tf_op jit(solution)/shard_map/psum | solution.py:107
  104.5 9.8 %psum.15 = f32[16]{0:T(128)S(1)} all-reduce(f32[16]{0:T(128)S(1)} %multiply_reduce_fusion), channel_id=1, replica_groups=mesh['groups'=2,'expert'=4,'tensor'=4] {'expert'}, use_global_device_ids=true, to_apply=%region_10.11 | all-reduce | flops 16 | bytes 128 | tf_op jit(solution)/shard_map/psum | solution.py:109
  114.4 0.7 gather_fusion.1
  115.1 0.7 broadcast_select_fusion.1
  115.8 3.3 %all-to-all-start.1 = ((bf16[4,12,1024]{2,1,0:T(8,128)(2,1)}), bf16[4,12,1024]{2,1,0:T(8,128)(2,1)S(1)}, u32[]{:S(2)}, u32[]{:S(2)}) async-start(bf16[4,12,1024]{2,1,0:T(8,128)(2,1)} %broadcast_select_fusion.1), calls=%async_computation.1 | async-start | bytes 262144 | tf_op jit(solution)/shard_map/all_to_all | solution.py:138
  119.2 0.2 reduce-scatter.2.cloned.1.call-start
  119.4 5.6 %all-to-all-done.1 = bf16[4,12,1024]{2,1,0:T(8,128)(2,1)S(1)} async-done(((bf16[4,12,1024]{2,1,0:T(8,128)(2,1)}), bf16[4,12,1024]{2,1,0:T(8,128)(2,1)S(1)}, u32[]{:S(2)}, u32[]{:S(2)}) %all-to-all-start.1) | async-done | bytes 98336 | tf_op jit(solution)/shard_map/all_to_all | solution.py:138
  125.2 8.0 %fusion.4 = f32[12,2048]{1,0:T(8,128)S(1)} fusion(bf16[12,4096]{1,0:T(8,128)(2,1)S(1)} %bitcast.60, bf16[1,4096,2048]{2,1,0:T(8,128)(2,1)} %param.23), kind=kOutput, calls=%fused_computation.7 | convolution fusion | flops 201326592 | bytes 16973824 | tf_op jit(solution)/shard_map/dot_general | solution.py:139
  133.3 13.0 %fusion = f32[12,4096]{1,0:T(8,128)S(1)} fusion(bf16[1,2048,4096]{2,1,0:T(8,128)(2,1)} %param.25, bf16[12,4096]{1,0:T(8,128)(2,1)S(1)} %bitcast.61, bf16[1,4096,2048]{2,1,0:T(8,128)(2,1)} %param.24, f32[12,2048]{1,0:T(8,128)S(1)} %fusion.4), kind=kOutput, calls=%fused_computation.3 | convolution fusion | flops 402800640 | bytes 33947648 | tf_op jit(solution)/shard_map/dot_general | solution.py:142
  146.3 0.6 gather_fusion.2
  147.0 0.7 multiply_convert_fusion
  147.7 0.6 dynamic-slice
  149.0 17.5 %reduce-scatter.2.cloned.1.call-done = bf16[16,1024]{1,0:T(8,128)(2,1)} async-done(((bf16[16,4096]{1,0:T(8,128)(2,1)}), bf16[16,1024]{1,0:T(8,128)(2,1)}) %reduce-scatter.2.cloned.1.call-update) | async-done | bytes 32784 | tf_op jit(solution)/shard_map/reduce_scatter | solution.py:148
  166.5 10.8 %all-reduce.2 = bf16[16,1024]{1,0:T(8,128)(2,1)S(1)} all-reduce(bf16[16,1024]{1,0:T(8,128)(2,1)} %reduce-scatter.2.cloned.1.call-done), channel_id=3, replica_groups=mesh['groups'=2,'expert'=4,'tensor'=4] {'tensor'}, use_global_device_ids=true, to_apply=%region_13.14.clone | all-reduce | flops 16384 | bytes 65536
  177.3 0.6 constant_dynamic-slice_fusion
  (64 shorter events, 2.0 us)
Async XLA Ops:
  7.2 1.6 copy-start
  19.5 6.5 %copy-start.5 = (bf16[4,1024]{1,0:T(4,128)(2,1)S(1)}, bf16[4,1024]{1,0:T(4,128)(2,1)}, u32[]{:S(2)}) copy-start(bf16[4,1024]{1,0:T(4,128)(2,1)} %param.16) | copy-start | bytes 24580
  19.5 6.5 %copy-start.4 = (bf16[4,2,256]{2,1,0:T(2,128)(2,1)S(1)}, bf16[4,2,256]{2,1,0:T(2,128)(2,1)}, u32[]{:S(2)}) copy-start(bf16[4,2,256]{2,1,0:T(2,128)(2,1)} %param.17) | copy-start | bytes 12292
  19.5 6.6 %copy-start.7 = (bf16[1024]{0:T(1024)(128)(2,1)S(1)}, bf16[1024]{0:T(1024)(128)(2,1)}, u32[]{:S(2)}) copy-start(bf16[1024]{0:T(1024)(128)(2,1)} %param.20) | copy-start | bytes 6148
  19.5 6.6 %copy-start.6 = (s32[16,2]{0,1:T(2,128)S(1)}, s32[16,2]{0,1:T(2,128)}, u32[]{:S(2)}) copy-start(s32[16,2]{0,1:T(2,128)} %param.21) | copy-start | bytes 388
  19.5 8.0 %copy-start.9 = (s32[16]{0:T(128)S(1)}, s32[16]{0:T(128)}, u32[]{:S(2)}) copy-start(s32[16]{0:T(128)} %param.15) | copy-start | bytes 196
  19.5 8.1 %copy-start.8 = (f32[16,2]{0,1:T(2,128)S(1)}, f32[16,2]{0,1:T(2,128)}, u32[]{:S(2)}) copy-start(f32[16,2]{0,1:T(2,128)} %param.22) | copy-start | bytes 388
  19.5 54.7 %all-to-all-start = ((bf16[16,128,2,256]{3,2,1,0:T(2,128)(2,1)}), bf16[16,128,2,256]{3,2,1,0:T(2,128)(2,1)S(1)}, u32[]{:S(2)}, u32[]{:S(2)}) async-start(bf16[16,128,2,256]{3,2,1,0:T(2,128)(2,1)} %broadcast_select_fusion), calls=%async_computation | async-start | bytes 4194304 | tf_op jit(solution)/shard_map/all_to_all | solution.py:93
  78.3 26.1 %copy-start.3 = (bf16[16,1024]{1,0:T(8,128)(2,1)S(1)}, bf16[16,1024]{1,0:T(8,128)(2,1)}, u32[]{:S(2)}) copy-start(bf16[16,1024]{1,0:T(8,128)(2,1)} %param.19) | copy-start | bytes 98308
  104.3 28.9 %copy-start.2 = (bf16[16,1024]{1,0:T(8,128)(2,1)}, bf16[16,1024]{1,0:T(8,128)(2,1)S(1)}, u32[]{:S(2)}) copy-start(bf16[16,1024]{1,0:T(8,128)(2,1)S(1)} %psum.14) | copy-start | bytes 98308
  115.8 9.2 %all-to-all-start.1 = ((bf16[4,12,1024]{2,1,0:T(8,128)(2,1)}), bf16[4,12,1024]{2,1,0:T(8,128)(2,1)S(1)}, u32[]{:S(2)}, u32[]{:S(2)}) async-start(bf16[4,12,1024]{2,1,0:T(8,128)(2,1)} %broadcast_select_fusion.1), calls=%async_computation.1 | async-start | bytes 262144 | tf_op jit(solution)/shard_map/all_to_all | solution.py:138
  119.2 47.3 %reduce-scatter.2.cloned.1.call-start = ((), (), s32[]{:S(2)}) async-start(), calls=%async_computation.3 | async-start | bytes 163840 | tf_op jit(solution)/shard_map/reduce_scatter | solution.py:148
  133.3 44.6 %copy-start.1 = (bf16[16,128,2,256]{3,2,1,0:T(2,128)(2,1)S(1)}, bf16[16,128,2,256]{3,2,1,0:T(2,128)(2,1)}, u32[]{:S(2)}) copy-start(bf16[16,128,2,256]{3,2,1,0:T(2,128)(2,1)} %param.13) | copy-start | bytes 6291460
  146.3 1.4 copy-start.10
Sparse Core Ops, SparseCore 0:
  147.8 18.6 reduce-scatter.1
where the time goes:
time: 185 us
  waiting for transfers between devices  69.6 us (38%)
  blocking collectives  44 us (24%)
  matrix products  23.9 us (13%)
  between operations  15 us (8%)
  local copies, waits for them, and re-layouts  13.1 us (7%)
  starting transfers between devices  10 us (5%)
  other arithmetic  9.12 us (5%)
    all_to_all x1, waiting for transfers between devices, shards(): lax.all_to_all(ordered, 'expert', split_axis=0, concat_axis=1, tiled=True)  46.4 us
    reduce_scatter x1, waiting for transfers between devices, shards(): lax.psum_scatter(contrib.astype(jnp.bfloat16), 'expert', scatter_dimensio...  17.5 us
    all_gather x1, blocking collectives, shards(): lax.all_gather(context, 'expert', axis=0, tiled=True)  13.2 us
    dot_general x1, matrix products, shards(): produced = jnp.dot(activated, down_slab, preferred_element_type=jnp.float32)  13 us
    unnamed x1, blocking collectives  10.8 us
    psum x1, blocking collectives, shards(): attention = lax.psum(partial_out.astype(jnp.bfloat16), 'tensor')  10.3 us
    psum x1, blocking collectives, shards(): lax.psum(jnp.sum(hidden_activation * hidden_activation, axis=1), 'expert')  9.82 us
    dot_general x1, matrix products, shards(): gate_sum = jnp.dot(arrived, gate_slab, preferred_element_type=jnp.float32)  8.04 us
  transfers between devices with their start and end apart: 3, of which 3 were waited for; matrix products, arithmetic and copies ran while one was open for 1% of the time, Pallas kernels for 0%

commit v1 on v0

--- a/solution.py
+++ b/solution.py
@@ -1,8 +1,11 @@
+import functools
 import math
 
 import jax
 import jax.numpy as jnp
 from jax import lax
+from jax.experimental import pallas as pl
+from jax.experimental.pallas import tpu as pltpu
 from jax.sharding import PartitionSpec as P
 
 D = 4096
@@ -155,9 +158,414 @@
     return (attention, moe_out)
 
 
+MESH = pl.DeviceIdType.MESH
+
+
+def remote(source, target, sems, index, where):
+    return pltpu.make_async_remote_copy(
+        src_ref=source,
+        dst_ref=target,
+        send_sem=sems.at[0, index],
+        recv_sem=sems.at[1, index],
+        device_id=where,
+        device_id_type=MESH,
+    )
+
+
+def fused_kernel(
+    experts_n,
+    tensor_n,
+    slot_ref,
+    len_ref,
+    q_ref,
+    new_ref,
+    resid_ref,
+    gain_ref,
+    ids_ref,
+    logits_ref,
+    kv_hbm,
+    wo_hbm,
+    wg_hbm,
+    wu_hbm,
+    wd_hbm,
+    attn_ref,
+    moe_ref,
+    kv_v,
+    wo_v,
+    wg_v,
+    wu_v,
+    wd_v,
+    qall,
+    head_rows,
+    pacc,
+    pstat,
+    abuf,
+    hbuf,
+    ssq,
+    gacc,
+    uacc,
+    act,
+    sbuf,
+    rbuf,
+    load_sem,
+    wg_sem,
+    wu_sem,
+    wd_sem,
+    q_sem,
+    pacc_sem,
+    pstat_sem,
+    a_sem,
+    h_sem,
+    ssq_sem,
+    r_sem,
+):
+    e = lax.axis_index("expert")
+    t = lax.axis_index("tensor")
+    own_seqs = q_ref.shape[0]
+    seqs = own_seqs * experts_n
+    heads = q_ref.shape[1] // HD
+    kv_local = new_ref.shape[2] // HD
+    group_size = heads // kv_local
+    keys2 = kv_v.shape[1]
+    positions = keys2 // 2
+    cols = wo_v.shape[1]
+    scale = 1.0 / math.sqrt(HD)
+    f32 = jnp.float32
+    bf16 = jnp.bfloat16
+
+    kv_load = pltpu.make_async_copy(kv_hbm, kv_v, load_sem.at[0])
+    kv_load.start()
+    wo_load = pltpu.make_async_copy(wo_hbm, wo_v, load_sem.at[1])
+    wo_load.start()
+
+    def column_block(step, sign):
+        return lax.rem(e + sign * step + experts_n, experts_n) * cols
+
+    gate_loads, up_loads, down_loads = [], [], []
+    for step in range(experts_n):
+        rows = pl.ds(pl.multiple_of(column_block(step, -1), 128), cols)
+        for hbm, vmem, sem, loads in (
+            (wg_hbm, wg_v, wg_sem, gate_loads),
+            (wu_hbm, wu_v, wu_sem, up_loads),
+        ):
+            load = pltpu.make_async_copy(hbm.at[0, rows, :], vmem.at[rows, :], sem.at[step])
+            load.start()
+            loads.append(load)
+    down_order = list(range(1, experts_n)) + [0]
+    for step in down_order:
+        block = pl.ds(pl.multiple_of(column_block(step, 1), 128), cols)
+        load = pltpu.make_async_copy(
+            wd_hbm.at[0, :, block], wd_v.at[:, block], wd_sem.at[step]
+        )
+        load.start()
+        down_loads.append(load)
+
+    barrier = pltpu.get_barrier_semaphore()
+    for k in range(1, experts_n * tensor_n):
+        where = {
+            "expert": lax.rem(e + k // tensor_n, experts_n),
+            "tensor": lax.rem(t + k % tensor_n, tensor_n),
+        }
+        pl.semaphore_signal(barrier, inc=1, device_id=where, device_id_type=MESH)
+    pl.semaphore_wait(barrier, experts_n * tensor_n - 1)
+
+    sends = []
+    q_copies = []
+    for step in range(1, experts_n):
+        copy = remote(
+            q_ref, qall.at[e], q_sem, step, {"expert": lax.rem(e + step, experts_n)}
+        )
+        copy.start()
+        q_copies.append(copy)
+    qall[e] = q_ref[...]
+    kv_load.wait()
+    for copy in q_copies:
+        copy.wait_recv()
+    for owner in range(experts_n):
+        block = qall[owner].astype(f32)
+        for h in range(heads):
+            head_rows[pl.ds(owner * own_seqs * heads + h, own_seqs, stride=heads), :] = block[
+                :, h * HD : (h + 1) * HD
+            ]
+
+    row_of = lax.broadcasted_iota(jnp.int32, (heads, HD), 0)
+    column = lax.broadcasted_iota(jnp.int32, (heads, keys2), 1)
+    is_key = lax.rem(column, 2) == 0
+    position = e * positions + lax.div(column, 2)
+
+    def by_group(pieces):
+        picked = pieces[0]
+        for g in range(1, kv_local):
+            picked = jnp.where(row_of >= g * group_size, pieces[g], picked)
+        return picked
+
+    score_list, live_list, own_list, value_list = [], [], [], []
+    for b in range(seqs):
+        q_rows = head_rows[b * heads : (b + 1) * heads, :]
+        spread = jnp.concatenate(
+            [
+                jnp.where(lax.div(row_of, group_size) == g, q_rows, 0.0)
+                for g in range(kv_local)
+            ],
+            axis=1,
+        ).astype(bf16)
+        cache = kv_v[slot_ref[b]]
+        raw = lax.dot_general(
+            spread, cache, (((1,), (1,)), ((), ())), preferred_element_type=f32
+        )
+        live = is_key & (position < len_ref[b])
+        score_list.append(jnp.where(live, raw * scale, MASKED))
+        live_list.append(jnp.where(live, 1.0, 0.0))
+        fresh = new_ref[b % own_seqs].astype(f32)
+        fresh_keys = by_group([fresh[0:1, g * HD : (g + 1) * HD] for g in range(kv_local)])
+        own = jnp.sum(q_rows * fresh_keys, axis=1, keepdims=True) * scale
+        own_list.append(jnp.where(e == b // own_seqs, own, MASKED))
+        value_list.append(
+            jnp.broadcast_to(
+                by_group([fresh[1:2, g * HD : (g + 1) * HD] for g in range(kv_local)]),
+                (heads, HD),
+            )
+        )
+    scores = jnp.concatenate(score_list, axis=0)
+    live = jnp.concatenate(live_list, axis=0)
+    own = jnp.concatenate(own_list, axis=0)
+    peak = jnp.maximum(jnp.max(scores, axis=1, keepdims=True), own)
+    weights = jnp.exp(scores - peak) * live
+    own_weight = jnp.where(own > 0.5 * MASKED, jnp.exp(own - peak), 0.0)
+    total = jnp.sum(weights, axis=1, keepdims=True) + own_weight
+    shifted = pltpu.roll(weights, 1, 1).astype(bf16)
+    for b in range(seqs):
+        out = jnp.dot(
+            shifted[b * heads : (b + 1) * heads, :],
+            kv_v[slot_ref[b]],
+            preferred_element_type=f32,
+        )
+        picked = by_group([out[:, g * HD : (g + 1) * HD] for g in range(kv_local)])
+        picked = picked + own_weight[b * heads : (b + 1) * heads] * value_list[b]
+        head_rows[b * heads : (b + 1) * heads, :] = picked
+    pacc[0] = head_rows[...].astype(bf16)
+    lane = lax.broadcasted_iota(jnp.int32, (seqs * heads, HD), 1)
+    stats = jnp.where(lane == 0, peak, jnp.where(lane == 1, total, 0.0))
+    pstat[0] = stats.T[0:8, :]
+
+    p_copies = []
+    for step in range(1, experts_n):
+        where = {"expert": lax.rem(e + step, experts_n)}
+        for buffer, sem in ((pstat, pstat_sem), (pacc, pacc_sem)):
+            copy = remote(buffer.at[0], buffer.at[step], sem, step, where)
+            copy.start()
+            p_copies.append(copy)
+
+    logits = logits_ref[...]
+    first_share = 1.0 / (1.0 + jnp.exp(logits[:, 1:2] - logits[:, 0:1]))
+    ids = ids_ref[...]
+    mix = jnp.where(ids[:, 0:1] == e, first_share, 0.0) + jnp.where(
+        ids[:, 1:2] == e, 1.0 - first_share, 0.0
+    )
+
+    wo_load.wait()
+    for copy in p_copies:
+        copy.wait_recv()
+    peaks = [pstat[j][0:1, :] for j in range(experts_n)]
+    top = functools.reduce(jnp.maximum, peaks)
+    factors = [jnp.exp(p - top) for p in peaks]
+    whole = sum(f * pstat[j][1:2, :] for j, f in enumerate(factors))
+    row8 = lax.broadcasted_iota(jnp.int32, (8, seqs * heads), 0)
+    stacked = jnp.zeros((8, seqs * heads), f32)
+    for j, f in enumerate(factors):
+        stacked = jnp.where(row8 == j, f / whole, stacked)
+    turned = stacked.T
+    context = sum(pacc[j].astype(f32) * turned[:, j : j + 1] for j in range(experts_n))
+    head_rows[...] = context
+    context = jnp.concatenate(
+        [head_rows[pl.ds(h, seqs, stride=heads), :] for h in range(heads)], axis=1
+    ).astype(bf16)
+    abuf[t] = jnp.dot(context, wo_v[...], preferred_element_type=f32).astype(bf16)
+
+    a_copies = []
+    for step in range(1, tensor_n):
+        copy = remote(
+            abuf.at[t], abuf.at[t], a_sem, step, {"tensor": lax.rem(t + step, tensor_n)}
+        )
+        copy.start()
+        a_copies.append(copy)
+    for copy in a_copies:
+        copy.wait_recv()
+    attention = sum(abuf[j].astype(f32) for j in range(tensor_n)).astype(bf16)
+    attn_ref[...] = attention
+    hidden = resid_ref[...].astype(f32) + attention.astype(f32)
+    hbuf[0] = (hidden * gain_ref[...].astype(f32)).astype(bf16)
+    ssq[0] = jnp.broadcast_to(jnp.sum(hidden * hidden, axis=1, keepdims=True), ssq.shape[1:])
+    h_copies, s_copies = [None], [None]
+    for step in range(1, experts_n):
+        where = {"expert": lax.rem(e + step, experts_n)}
+        copy = remote(hbuf.at[0], hbuf.at[step], h_sem, step, where)
+        copy.start()
+        h_copies.append(copy)
+        copy = remote(ssq.at[0], ssq.at[step], ssq_sem, step, where)
+        copy.start()
+        s_copies.append(copy)
+
+    hidden_units = wg_v.shape[1]
+    width = math.gcd(hidden_units, 512)
+    for step in range(experts_n):
+        if step:
+            h_copies[step].wait_recv()
+        gate_loads[step].wait()
+        up_loads[step].wait()
+        rows = pl.ds(pl.multiple_of(column_block(step, -1), 128), cols)
+        tokens = hbuf[step]
+
+        def one(i, carry, rows=rows, tokens=tokens, step=step):
+            block = pl.ds(pl.multiple_of(i * width, width), width)
+            gate = jnp.dot(tokens, wg_v[rows, block], preferred_element_type=f32)
+            up = jnp.dot(tokens, wu_v[rows, block], preferred_element_type=f32)
+            if step:
+                gate = gate + gacc[:, block]
+                up = up + uacc[:, block]
+            gacc[:, block] = gate
+            uacc[:, block] = up
+            return carry
+
+        lax.fori_loop(0, hidden_units // width, one, 0)
+    for step in range(1, experts_n):
+        s_copies[step].wait_recv()
+    squares = sum(ssq[j][:, 0:1] for j in range(experts_n))
+    inverse = lax.rsqrt(squares / (cols * experts_n) + EPSILON)
+    gate = gacc[...] * inverse
+    up = uacc[...] * inverse
+    act[...] = (gate / (1.0 + jnp.exp(-gate)) * up).astype(bf16)
+
+    out_rows = seqs // tensor_n
+    down_width = math.gcd(cols, 512)
+    r_copies = []
+    for step, load in zip(down_order, down_loads):
+        load.wait()
+        start = column_block(step, 1)
+
+        def one_down(i, carry, start=start, step=step):
+            offset = pl.multiple_of(i * down_width, down_width)
+            block = pl.ds(pl.multiple_of(start + offset, 128), down_width)
+            made = jnp.dot(act[...], wd_v[:, block], preferred_element_type=f32) * mix
+            for p in range(tensor_n):
+                sbuf[step, p, :, pl.ds(offset, down_width)] = made[
+                    p * out_rows : (p + 1) * out_rows
+                ].astype(bf16)
+            return carry
+
+        lax.fori_loop(0, cols // down_width, one_down, 0)
+        for turn in range(tensor_n):
+            if step == 0 and turn == 0:
+                continue
+            k = step * tensor_n + turn
+            target = lax.rem(t + turn, tensor_n)
+            where = {"expert": lax.rem(e + step, experts_n), "tensor": target}
+            copy = remote(sbuf.at[step, target], rbuf.at[k], r_sem, k, where)
+            copy.start()
+            r_copies.append(copy)
+    result = sbuf[0, t].astype(f32)
+    for copy in r_copies:
+        copy.wait_recv()
+    for k in range(1, experts_n * tensor_n):
+        result = result + rbuf[k].astype(f32)
+    moe_ref[...] = result.astype(bf16)
+    for copy in (
+        q_copies + p_copies + a_copies + h_copies[1:] + s_copies[1:] + r_copies
+    ):
+        copy.wait_send()
+
+
+def fused(
+    kv_prefill, slot_of, lengths, query, new_kv, wo, resid, norm_gain, expert_ids,
+    gate_logits, gate_weight_slabs, w_up, w_down,
+):
+    experts_n = lax.axis_size("expert")
+    tensor_n = lax.axis_size("tensor")
+    slots, positions, _, kv_cols = kv_prefill.shape
+    own_seqs = query.shape[0]
+    seqs = lengths.shape[0]
+    cols = resid.shape[1]
+    heads = query.shape[1] // HD
+    hidden_units = w_down.shape[1]
+    out_rows = seqs // tensor_n
+    bf16 = jnp.bfloat16
+    f32 = jnp.float32
+    vmem = pl.BlockSpec(memory_space=pltpu.VMEM)
+    smem = pl.BlockSpec(memory_space=pltpu.SMEM)
+    hbm = pl.BlockSpec(memory_space=pl.ANY)
+    dma = pltpu.SemaphoreType.DMA
+    peers = experts_n * tensor_n
+    return tuple(
+        pl.pallas_call(
+            functools.partial(fused_kernel, experts_n, tensor_n),
+            out_shape=(
+                jax.ShapeDtypeStruct((seqs, cols), bf16),
+                jax.ShapeDtypeStruct((out_rows, cols), bf16),
+            ),
+            in_specs=[smem, smem] + [vmem] * 6 + [hbm] * 5,
+            out_specs=(vmem, vmem),
+            scratch_shapes=[
+                pltpu.VMEM((slots, positions * 2, kv_cols), bf16),
+                pltpu.VMEM(wo.shape, bf16),
+                pltpu.VMEM(gate_weight_slabs.shape[1:], bf16),
+                pltpu.VMEM(w_up.shape[1:], bf16),
+                pltpu.VMEM(w_down.shape[1:], bf16),
+                pltpu.VMEM((experts_n,) + query.shape, bf16),
+                pltpu.VMEM((seqs * heads, HD), f32),
+                pltpu.VMEM((experts_n, seqs * heads, HD), bf16),
+                pltpu.VMEM((experts_n, 8, seqs * heads), f32),
+                pltpu.VMEM((tensor_n, seqs, cols), bf16),
+                pltpu.VMEM((experts_n, seqs, cols), bf16),
+                pltpu.VMEM((experts_n, seqs, 128), f32),
+                pltpu.VMEM((seqs, hidden_units), f32),
+                pltpu.VMEM((seqs, hidden_units), f32),
+                pltpu.VMEM((seqs, hidden_units), bf16),
+                pltpu.VMEM((experts_n, tensor_n, out_rows, cols), bf16),
+                pltpu.VMEM((peers, out_rows, cols), bf16),
+                dma((2,)),
+                dma((experts_n,)),
+                dma((experts_n,)),
+                dma((experts_n,)),
+                dma((2, experts_n)),
+                dma((2, experts_n)),
+                dma((2, experts_n)),
+                dma((2, tensor_n)),
+                dma((2, experts_n)),
+                dma((2, experts_n)),
+                dma((2, peers)),
+            ],
+            compiler_params=pltpu.CompilerParams(
+                collective_id=0, has_side_effects=True, vmem_limit_bytes=60 * 1024 * 1024
+            ),
+        )(
+            slot_of, lengths, query, new_kv, resid, norm_gain.reshape(1, cols), expert_ids,
+            gate_logits, kv_prefill.reshape(slots, positions * 2, kv_cols), wo,
+            gate_weight_slabs, w_up, w_down,
+        )
+    )
+
+
+def layer(*arrays):
+    kv_prefill, slot_of, lengths, query = arrays[:4]
+    gate_slabs = arrays[10]
+    weights = 3 * gate_slabs.size * 2
+    rows = lengths.shape[0] * (query.shape[1] // HD)
+    if (
+        lax.axis_size("expert") == EXPERTS
+        and gate_slabs.shape[0] == 1
+        and (2 * kv_prefill.shape[1]) % 128 == 0
+        and (query.shape[1] // HD) % 8 == 0
+        and lengths.shape[0] % 16 == 0
+        and rows == 128
+        and weights <= 52 * 2**20
+    ):
+        return fused(*arrays)
+    return shards(*arrays)
+
+
 def solution(mesh):
     return jax.shard_map(
-        shards,
+        layer,
         mesh=mesh,
         in_specs=(
             P("groups", "expert", None, "tensor"),

time: 185 us -> 47.7 us (0.26)
  waiting for transfers between devices: 69.6 us -> 0 us
  blocking collectives: 44 us -> 0 us
  Pallas kernels: 0 us -> 35.9 us
  matrix products: 23.9 us -> 0 us
  between operations: 15 us -> 0.64 us
  starting transfers between devices: 10 us -> 0 us
  other arithmetic: 9.12 us -> 0 us
  local copies, waits for them, and re-layouts: 13.1 us -> 10.8 us
    all_to_all x2 -> x0, waiting for transfers between devices: 52 us -> none  [the longest x1 46.4 us: shards(): lax.all_to_all(ordered, 'expert', split_axis=0, concat_axis=1, tiled=True)]
    pallas_call x0 -> x1, Pallas kernels: none -> 35.9 us  [fused(): pl.pallas_call(functools.partial(fused_kernel, experts_n, tensor_n), out_...]
    dot_general x6 -> x0, matrix products: 23.9 us -> none  [the longest x1 13 us: shards(): produced = jnp.dot(activated, down_slab, preferred_element_type=jnp.float32)]
    psum x2 -> x0, blocking collectives: 20.1 us -> none  [the longest x1 10.3 us: shards(): attention = lax.psum(partial_out.astype(jnp.bfloat16), 'tensor')]
    reduce_scatter x1 -> x0, waiting for transfers between devices: 17.5 us -> none  [shards(): lax.psum_scatter(contrib.astype(jnp.bfloat16), 'expert', scatter_dimensio...]
    all_gather x1 -> x0, blocking collectives: 13.2 us -> none  [shards(): lax.all_gather(context, 'expert', axis=0, tiled=True)]
    unnamed x1 -> x0, blocking collectives: 10.8 us -> none
    all_to_all x2 -> x0, starting transfers between devices: 9.81 us -> none  [the longest x1 6.49 us: shards(): lax.all_to_all(ordered, 'expert', split_axis=0, concat_axis=1, tiled=True)]
  transfers between devices with their start and end apart: 3 -> 0, of which waited for: 3 -> 0; matrix products, arithmetic and copies ran while one was open for 1% -> 0% of each run, Pallas kernels for 0% -> 0%
where the time goes in v1:
time: 47.7 us; the launch traced here: 47.3 us
  Pallas kernels  35.9 us (75%)
  local copies, waits for them, and re-layouts  10.8 us (23%)
  between operations  0.64 us (1%)
    pallas_call x1, Pallas kernels, fused(): pl.pallas_call(functools.partial(fused_kernel, experts_n, tensor_n), out_...  35.9 us
    unnamed x4, local copies, waits for them, and re-layouts  5.38 us
    reshape x1, local copies, waits for them, and re-layouts, fused(): kv_prefill.reshape(slots, positions * 2, kv_cols)  4.11 us
    reshape x1, local copies, waits for them, and re-layouts, fused(): norm_gain.reshape(1, cols)  1.28 us

profile of v1, /device:TPU:0, one launch (start us, length us, event | category | flops | bytes accessed | tf_op | source)
XLA Modules:
  0.0 47.3 jit_solution(17609154650457161232)
XLA Ops:
  0.6 1.3 %reshape.10.gain_ref = bf16[1,1024]{1,0:T(2,128)(2,1)} reshape(bf16[1024]{0:T(1024)(128)(2,1)} %param.20) | data formatting | bytes 4096 | tf_op jit(solution)/shard_map/reshape | solution.py:541
  1.9 1.4 %copy.15.ids_ref = s32[16,2]{1,0:T(8,128)} copy(s32[16,2]{0,1:T(2,128)} %param.21) | data formatting | bytes 256 | tf_op args[8]
  3.3 1.4 %copy.16.logits_ref = f32[16,2]{1,0:T(8,128)} copy(f32[16,2]{0,1:T(2,128)} %param.22) | data formatting | bytes 256 | tf_op args[9]
  4.6 4.1 %reshape.11.kv_hbm = bf16[16,256,256]{2,1,0:T(8,128)(2,1)} reshape(bf16[16,128,2,256]{3,2,1,0:T(2,128)(2,1)} %param.13) | data formatting | bytes 4194304 | tf_op jit(solution)/shard_map/reshape | solution.py:542
  8.7 35.9 %shard_map.140 = (bf16[16,1024]{1,0:T(8,128)(2,1)}, bf16[4,1024]{1,0:T(4,128)(2,1)}) custom-call(s32[16]{0:T(128)} %slot_ref.1, s32[16]{0:T(128)} %len_ref.1, bf16[4,1024]{1,0:T(4,128)(2,1)} %q_ref.1, bf16[4,2,256]{2,1,0:T(2,128)(2,1)} %new_ref.1, bf16[16,1024]{1,0:T(8,128)(2,1)} %resid_ref.1, bf16[1,1024]{1,0:T(2,128)(2,1)} %reshape.10.gain_ref, ...), custom_call_target="tpu_custom_call" | custom-call | tf_op jit(solution)/shard_map/pallas_call | solution.py:499
  44.6 1.4 %copy.19 = bf16[16,1024]{1,0:T(8,128)(2,1)} copy(bf16[16,1024]{1,0:T(8,128)(2,1)} %get-tuple-element.4) | data formatting | bytes 65536
  46.0 1.3 %copy.20 = bf16[4,1024]{1,0:T(4,128)(2,1)} copy(bf16[4,1024]{1,0:T(4,128)(2,1)} %get-tuple-element.5) | data formatting | bytes 16384

commit v2 on v1

--- a/solution.py
+++ b/solution.py
@@ -226,16 +226,17 @@
     heads = q_ref.shape[1] // HD
     kv_local = new_ref.shape[2] // HD
     group_size = heads // kv_local
-    keys2 = kv_v.shape[1]
-    positions = keys2 // 2
+    positions = kv_v.shape[1]
+    keys2 = 2 * positions
+    kv_flat = kv_v.reshape(kv_v.shape[0], keys2, kv_v.shape[3])
     cols = wo_v.shape[1]
     scale = 1.0 / math.sqrt(HD)
     f32 = jnp.float32
     bf16 = jnp.bfloat16
 
-    kv_load = pltpu.make_async_copy(kv_hbm, kv_v, load_sem.at[0])
+    kv_load = pltpu.make_async_copy(kv_hbm, kv_v, load_sem.at[1])
     kv_load.start()
-    wo_load = pltpu.make_async_copy(wo_hbm, wo_v, load_sem.at[1])
+    wo_load = pltpu.make_async_copy(wo_hbm, wo_v, load_sem.at[0])
     wo_load.start()
 
     def column_block(step, sign):
@@ -299,7 +300,7 @@
             picked = jnp.where(row_of >= g * group_size, pieces[g], picked)
         return picked
 
-    score_list, live_list, own_list, value_list = [], [], [], []
+    cache_list, score_list, live_list, own_list, value_list = [], [], [], [], []
     for b in range(seqs):
         q_rows = head_rows[b * heads : (b + 1) * heads, :]
         spread = jnp.concatenate(
@@ -309,9 +310,9 @@
             ],
             axis=1,
         ).astype(bf16)
-        cache = kv_v[slot_ref[b]]
+        cache_list.append(kv_flat[slot_ref[b]])
         raw = lax.dot_general(
-            spread, cache, (((1,), (1,)), ((), ())), preferred_element_type=f32
+            spread, cache_list[b], (((1,), (1,)), ((), ())), preferred_element_type=f32
         )
         live = is_key & (position < len_ref[b])
         score_list.append(jnp.where(live, raw * scale, MASKED))
@@ -337,7 +338,7 @@
     for b in range(seqs):
         out = jnp.dot(
             shifted[b * heads : (b + 1) * heads, :],
-            kv_v[slot_ref[b]],
+            cache_list[b],
             preferred_element_type=f32,
         )
         picked = by_group([out[:, g * HD : (g + 1) * HD] for g in range(kv_local)])
@@ -346,7 +347,7 @@
     pacc[0] = head_rows[...].astype(bf16)
     lane = lax.broadcasted_iota(jnp.int32, (seqs * heads, HD), 1)
     stats = jnp.where(lane == 0, peak, jnp.where(lane == 1, total, 0.0))
-    pstat[0] = stats.T[0:8, :]
+    pstat[0] = stats.T[0:2, :]
 
     p_copies = []
     for step in range(1, experts_n):
@@ -357,11 +358,15 @@
             p_copies.append(copy)
 
     logits = logits_ref[...]
-    first_share = 1.0 / (1.0 + jnp.exp(logits[:, 1:2] - logits[:, 0:1]))
+    first_share = 1.0 / (1.0 + jnp.exp(logits[1:2, :] - logits[0:1, :]))
     ids = ids_ref[...]
-    mix = jnp.where(ids[:, 0:1] == e, first_share, 0.0) + jnp.where(
-        ids[:, 1:2] == e, 1.0 - first_share, 0.0
-    )
+    mix_row = jnp.where(ids[0:1, :] == e, first_share, 0.0) + jnp.where(
+        ids[1:2, :] == e, 1.0 - first_share, 0.0
+    )
+    diagonal = lax.broadcasted_iota(jnp.int32, (seqs, seqs), 0) == lax.broadcasted_iota(
+        jnp.int32, (seqs, seqs), 1
+    )
+    mix = jnp.sum(jnp.where(diagonal, mix_row, 0.0), axis=1, keepdims=True)
 
     wo_load.wait()
     for copy in p_copies:
@@ -394,8 +399,14 @@
     attention = sum(abuf[j].astype(f32) for j in range(tensor_n)).astype(bf16)
     attn_ref[...] = attention
     hidden = resid_ref[...].astype(f32) + attention.astype(f32)
-    hbuf[0] = (hidden * gain_ref[...].astype(f32)).astype(bf16)
-    ssq[0] = jnp.broadcast_to(jnp.sum(hidden * hidden, axis=1, keepdims=True), ssq.shape[1:])
+    gain_rows = gain_ref[...].astype(f32)
+    gain = jnp.concatenate([gain_rows[i : i + 1, :] for i in range(gain_rows.shape[0])], axis=1)
+    hbuf[0] = (hidden * gain).astype(bf16)
+    square_sums = jnp.sum(hidden * hidden, axis=1, keepdims=True)
+    wide_diagonal = lax.broadcasted_iota(jnp.int32, (seqs, 128), 0) == lax.broadcasted_iota(
+        jnp.int32, (seqs, 128), 1
+    )
+    ssq[0] = jnp.sum(jnp.where(wide_diagonal, square_sums, 0.0), axis=0, keepdims=True)
     h_copies, s_copies = [None], [None]
     for step in range(1, experts_n):
         where = {"expert": lax.rem(e + step, experts_n)}
@@ -430,7 +441,8 @@
         lax.fori_loop(0, hidden_units // width, one, 0)
     for step in range(1, experts_n):
         s_copies[step].wait_recv()
-    squares = sum(ssq[j][:, 0:1] for j in range(experts_n))
+    square_row = sum(ssq[j] for j in range(experts_n))
+    squares = jnp.sum(jnp.where(wide_diagonal, square_row, 0.0), axis=1, keepdims=True)
     inverse = lax.rsqrt(squares / (cols * experts_n) + EPSILON)
     gate = gacc[...] * inverse
     up = uacc[...] * inverse
@@ -475,6 +487,11 @@
         copy.wait_send()
 
 
+def write_results(attention_ref, produced_ref, attn_ref, moe_ref):
+    attn_ref[...] = attention_ref[...]
+    moe_ref[...] = produced_ref[...]
+
+
 def fused(
     kv_prefill, slot_of, lengths, query, new_kv, wo, resid, norm_gain, expert_ids,
     gate_logits, gate_weight_slabs, w_up, w_down,
@@ -495,7 +512,7 @@
     hbm = pl.BlockSpec(memory_space=pl.ANY)
     dma = pltpu.SemaphoreType.DMA
     peers = experts_n * tensor_n
-    return tuple(
+    attention, produced = (
         pl.pallas_call(
             functools.partial(fused_kernel, experts_n, tensor_n),
             out_shape=(
@@ -505,7 +522,7 @@
             in_specs=[smem, smem] + [vmem] * 6 + [hbm] * 5,
             out_specs=(vmem, vmem),
             scratch_shapes=[
-                pltpu.VMEM((slots, positions * 2, kv_cols), bf16),
+                pltpu.VMEM(kv_prefill.shape, bf16),
                 pltpu.VMEM(wo.shape, bf16),
                 pltpu.VMEM(gate_weight_slabs.shape[1:], bf16),
                 pltpu.VMEM(w_up.shape[1:], bf16),
@@ -513,10 +530,10 @@
                 pltpu.VMEM((experts_n,) + query.shape, bf16),
                 pltpu.VMEM((seqs * heads, HD), f32),
                 pltpu.VMEM((experts_n, seqs * heads, HD), bf16),
-                pltpu.VMEM((experts_n, 8, seqs * heads), f32),
+                pltpu.VMEM((experts_n, 2, seqs * heads), f32),
                 pltpu.VMEM((tensor_n, seqs, cols), bf16),
                 pltpu.VMEM((experts_n, seqs, cols), bf16),
-                pltpu.VMEM((experts_n, seqs, 128), f32),
+                pltpu.VMEM((experts_n, 1, 128), f32),
                 pltpu.VMEM((seqs, hidden_units), f32),
                 pltpu.VMEM((seqs, hidden_units), f32),
                 pltpu.VMEM((seqs, hidden_units), bf16),
@@ -538,11 +555,21 @@
                 collective_id=0, has_side_effects=True, vmem_limit_bytes=60 * 1024 * 1024
             ),
         )(
-            slot_of, lengths, query, new_kv, resid, norm_gain.reshape(1, cols), expert_ids,
-            gate_logits, kv_prefill.reshape(slots, positions * 2, kv_cols), wo,
+            slot_of, lengths, query, new_kv, resid, norm_gain.reshape(cols // 128, 128), expert_ids.T,
+            gate_logits.T, kv_prefill, wo,
             gate_weight_slabs, w_up, w_down,
         )
     )
+
+    return pl.pallas_call(
+        write_results,
+        out_shape=(
+            jax.ShapeDtypeStruct(attention.shape, bf16),
+            jax.ShapeDtypeStruct(produced.shape, bf16),
+        ),
+        in_specs=[vmem, vmem],
+        out_specs=(vmem, vmem),
+    )(attention, produced)
 
 
 def layer(*arrays):

time: 47.7 us -> 38.1 us (0.80)
  local copies, waits for them, and re-layouts: 10.8 us -> 0 us
  Pallas kernels: 35.9 us -> 37.2 us
    reshape x2 -> x0, local copies, waits for them, and re-layouts: 5.38 us -> none  [the longest x1 4.11 us: fused(): kv_prefill.reshape(slots, positions * 2, kv_cols)]
    unnamed x4 -> x0, local copies, waits for them, and re-layouts: 5.38 us -> none
    pallas_call x0 -> x1, Pallas kernels: none -> 1.38 us  [fused(): pl.pallas_call(write_results, out_shape=(jax.ShapeDtypeStruct(attention.s...]
where the time goes in v2:
time: 38.1 us; the launch traced here: 37.9 us
  Pallas kernels  37.2 us (98%)
  between operations  0.64 us (2%)
    pallas_call x1, Pallas kernels, fused(): pl.pallas_call(functools.partial(fused_kernel, experts_n, tensor_n), out_...  35.9 us
    pallas_call x1, Pallas kernels, fused(): pl.pallas_call(write_results, out_shape=(jax.ShapeDtypeStruct(attention.s...  1.38 us

profile of v2, /device:TPU:0, one launch (start us, length us, event | category | flops | bytes accessed | tf_op | source)
XLA Modules:
  0.0 37.9 jit_solution(1614197663358252646)
XLA Ops:
  0.6 35.9 %shard_map.140 = (bf16[16,1024]{1,0:T(8,128)(2,1)}, bf16[4,1024]{1,0:T(4,128)(2,1)}) custom-call(s32[16]{0:T(128)} %slot_ref.1, s32[16]{0:T(128)} %len_ref.1, bf16[4,1024]{1,0:T(4,128)(2,1)} %q_ref.1, bf16[4,2,256]{2,1,0:T(2,128)(2,1)} %new_ref.1, bf16[16,1024]{1,0:T(8,128)(2,1)} %resid_ref.1, bf16[8,128]{1,0:T(8,128)(2,1)} %bitcast.3, s32[2,16]{1,0:T(2,128)} %bitcast.4, ...), custom_call_target="tpu_custom_call" | custom-call | tf_op jit(solution)/shard_map/pallas_call | solution.py:516
  36.5 1.4 %shard_map.141 = (bf16[16,1024]{1,0:T(8,128)(2,1)}, bf16[4,1024]{1,0:T(4,128)(2,1)}) custom-call(bf16[16,1024]{1,0:T(8,128)(2,1)} %get-tuple-element.4.attention_ref, bf16[4,1024]{1,0:T(4,128)(2,1)} %get-tuple-element.5.produced_ref), custom_call_target="tpu_custom_call" | custom-call | tf_op jit(solution)/shard_map/pallas_call | solution.py:564
